TPU v7x, 32 devices: a whole 2x2x4 slice. The times are simulated.
32 devices in a mesh: row: 8 (over z, core), col: 4 (over y, x).
Axes of the slice: x: 2, y: 2, z: 4, core: 2. Of those that a mesh axis runs over, the one named last changes fastest.
Arguments:
- fine_residual: float32 [16, 3, 1572864], P(None, None, ('row', 'col')), may hold values from -6 to 6
- restriction: float32 [3, 3, 1572864], P(None, None, ('row', 'col')), may hold values from -1.25 to 1.25
- restriction_pattern: int32 [1572864], P(('row', 'col')), may hold values 0 or 1
- cell_aggregate: int32 [384, 512], P('row', 'col'), may hold values from 0 to 196607, as said below
- block_inverse: float32 [3, 3, 384, 512], P(None, None, 'row', 'col'), may hold values from -4 to 4, as said below
- off_blocks: float32 [4, 3, 3, 384, 512], P(None, None, None, 'row', 'col'), may hold values from -0.5 to 0.5
- operator_pattern: int32 [4, 384, 512], P(None, 'row', 'col'), may hold values 0 or 1
Outputs:
- coarse_solution: float32 [16, 3, 384, 512], P(None, None, 'row', 'col')
- fine_correction: float32 [16, 3, 1572864], P(None, None, ('row', 'col'))
Inputs may be any that keep to these rules, and one draw needn't show every extreme that they name: `cell_aggregate`: every aggregate number 0 to 196607 stands in exactly one coarse cell. Aggregate g = f * 6144 + a lies in the tile numbered a mod 32, where the tile of rows i * 48 to (i + 1) * 48 - 1 and columns j * 128 to (j + 1) * 128 - 1 is numbered i * 4 + j. `block_inverse`: each 3x3 block is the inverse of a cell's diagonal block.
All inputs are finite; a program needn't handle non-finite values. No bound on the sum of `restriction_pattern` or of `operator_pattern` on one device may be relied on, other than what follows from the above.
Results may differ from a plain program's by a relative error of at most 0.00002.
Values sent between devices are 32-bit elements; how exact they have to be, the bound alone decides.
A program may use at most 128 MiB of HBM per device.

v0:
```python
import functools

import jax
import jax.numpy as jnp
from jax import lax
from jax.experimental import pallas as pl
from jax.experimental.pallas import tpu as pltpu
from jax.sharding import PartitionSpec as P

FPA = 8
ITERS = 4
AGG_DEV = 6144
LANES = 128
GROUP = 8
MESH = pl.DeviceIdType.MESH
VMEM_LIMIT = 56 * 1024 * 1024


def spec_vmem():
    return pl.BlockSpec(memory_space=pltpu.VMEM)


def restrict_kernel(devices, loads, *refs):
    residuals = refs[0:FPA]
    restrictions = refs[FPA : 2 * FPA]
    patterns = refs[2 * FPA : 3 * FPA]
    out_ref = refs[3 * FPA]
    stage = refs[3 * FPA + 1]
    group = pl.program_id(0)
    groups = AGG_DEV // (LANES * GROUP)
    parts = LANES // devices
    rows = 3 * groups * parts
    for block in range(GROUP):
        lanes = slice(block * LANES, (block + 1) * LANES)
        totals = [None, None, None]
        for p in range(FPA):
            present = patterns[p][block : block + 1, :].astype(jnp.float32)
            for j in range(3):
                masked = residuals[p][j, :, lanes] * present
                for i in range(3):
                    term = restrictions[p][i, j : j + 1, lanes] * masked
                    totals[i] = term if totals[i] is None else totals[i] + term
        for i in range(3):
            stage[i, block * loads : (block + 1) * loads, :] = totals[i]
    for i in range(3):
        turned = stage[i].T
        for part in range(parts):
            start = i * groups * parts + group * parts + part
            out_ref[pl.ds(start, devices, stride=rows), :] = turned[part * devices : (part + 1) * devices, :]


def restrict(residual, restriction, pattern, devices):
    loads = residual.shape[0]
    residual = residual.transpose(1, 0, 2)
    pattern = pattern.reshape(-1, LANES)
    width = LANES * GROUP
    groups = AGG_DEV // width
    rows = 3 * groups * (LANES // devices)
    res_specs = [pl.BlockSpec((3, loads, width), functools.partial(lambda p, g: (0, 0, p * groups + g), p)) for p in range(FPA)]
    rst_specs = [pl.BlockSpec((3, 3, width), functools.partial(lambda p, g: (0, 0, p * groups + g), p)) for p in range(FPA)]
    pat_specs = [pl.BlockSpec((GROUP, LANES), functools.partial(lambda p, g: (p * groups + g, 0), p)) for p in range(FPA)]
    return pl.pallas_call(
        functools.partial(restrict_kernel, devices, loads),
        grid=(groups,),
        in_specs=res_specs + rst_specs + pat_specs,
        out_specs=pl.BlockSpec((devices * rows, LANES), lambda g: (0, 0)),
        out_shape=jax.ShapeDtypeStruct((devices * rows, LANES), jnp.float32),
        scratch_shapes=[pltpu.VMEM((3, LANES, LANES), jnp.float32)],
        compiler_params=pltpu.CompilerParams(vmem_limit_bytes=VMEM_LIMIT),
        name="restrict",
    )(*([residual] * FPA + [restriction] * FPA + [pattern] * FPA))


def gather_kernel(devices, loads, slots_ref, chunk_ref, out_ref, table, staged):
    groups = AGG_DEV // (LANES * GROUP)
    piece = groups * (LANES // devices)
    lane = lax.broadcasted_iota(jnp.int32, (piece, LANES), 1)

    def unpack(f, carry):
        base = f * (3 * piece)
        parts = [chunk_ref[pl.ds(base + i * piece, piece), :] for i in range(3)]
        for block in range(GROUP):
            moved = []
            for i in range(3):
                shift = ((i - block) * loads) % LANES
                moved.append(pltpu.roll(parts[i], shift, 1) if shift else parts[i])
            row = jnp.where(lane < loads, moved[0], jnp.where(lane < 2 * loads, moved[1], moved[2]))
            table[pl.ds(f * (GROUP * piece) + block * piece, piece), :] = row
        return carry

    lax.fori_loop(0, devices, unpack, 0)
    height = out_ref.shape[0] // (3 * loads)

    def take(r, carry):
        for c in range(LANES):
            staged[pl.ds(c, 1), :] = table[pl.ds(slots_ref[r * LANES + c], 1), :]
        turned = staged[...].T
        out_ref[pl.ds(r, 3 * loads, stride=height), :] = turned[: 3 * loads, :]
        return carry

    lax.fori_loop(0, height, take, 0)


def gather(slots, chunks, devices, loads, height):
    return pl.pallas_call(
        functools.partial(gather_kernel, devices, loads),
        in_specs=[pl.BlockSpec(memory_space=pltpu.SMEM), spec_vmem()],
        out_specs=spec_vmem(),
        out_shape=jax.ShapeDtypeStruct((3 * loads * height, LANES), jnp.float32),
        scratch_shapes=[pltpu.VMEM((AGG_DEV, LANES), jnp.float32), pltpu.VMEM((LANES, LANES), jnp.float32)],
        compiler_params=pltpu.CompilerParams(vmem_limit_bytes=VMEM_LIMIT),
        name="gather_cells",
    )(slots, chunks)


def scatter_kernel(devices, loads, slots_ref, solution_ref, out_ref, table, staged):
    groups = AGG_DEV // (LANES * GROUP)
    piece = groups * (LANES // devices)
    height = solution_ref.shape[0] // (3 * loads)
    staged[...] = jnp.zeros_like(staged)

    def put(r, carry):
        staged[:, : 3 * loads] = solution_ref[pl.ds(r, 3 * loads, stride=height), :].T
        for c in range(LANES):
            table[pl.ds(slots_ref[r * LANES + c], 1), :] = staged[pl.ds(c, 1), :]
        return carry

    lax.fori_loop(0, height, put, 0)
    lane = lax.broadcasted_iota(jnp.int32, (piece, LANES), 1)

    def pack(f, carry):
        rows = [table[pl.ds(f * (GROUP * piece) + block * piece, piece), :] for block in range(GROUP)]
        for i in range(3):
            total = None
            for block in range(GROUP):
                shift = ((block - i) * loads) % LANES
                moved = pltpu.roll(rows[block], shift, 1) if shift else rows[block]
                total = moved if total is None else jnp.where(lane < block * loads, total, moved)
            out_ref[pl.ds(f * (3 * piece) + i * piece, piece), :] = total
        return carry

    lax.fori_loop(0, devices, pack, 0)


def scatter(slots, solution_planes, devices, loads):
    groups = AGG_DEV // (LANES * GROUP)
    piece = groups * (LANES // devices)
    return pl.pallas_call(
        functools.partial(scatter_kernel, devices, loads),
        in_specs=[pl.BlockSpec(memory_space=pltpu.SMEM), spec_vmem()],
        out_specs=spec_vmem(),
        out_shape=jax.ShapeDtypeStruct((devices * 3 * piece, LANES), jnp.float32),
        scratch_shapes=[pltpu.VMEM((AGG_DEV, LANES), jnp.float32), pltpu.VMEM((LANES, LANES), jnp.float32)],
        compiler_params=pltpu.CompilerParams(vmem_limit_bytes=VMEM_LIMIT),
        name="scatter_cells",
    )(slots, solution_planes)


def sweep_kernel(
    row_count,
    col_count,
    loads,
    rhs_ref,
    inverse_ref,
    blocks_ref,
    pattern_ref,
    out_ref,
    planes_ref,
    base,
    x,
    mixed,
    sent,
    halo,
    send_sem,
    recv_sem,
):
    height = inverse_ref.shape[2]
    planes = 3 * loads
    row = lax.axis_index("row")
    col = lax.axis_index("col")
    exists = (row > 0, row < row_count - 1, col > 0, col < col_count - 1)
    peers = (
        {"row": row - 1, "col": col},
        {"row": row + 1, "col": col},
        {"row": row, "col": col - 1},
        {"row": row, "col": col + 1},
    )
    barrier = pltpu.get_barrier_semaphore()
    halo[...] = jnp.zeros_like(halo)
    for d in range(4):

        @pl.when(exists[d])
        def _():
            pl.semaphore_signal(barrier, inc=1, device_id=peers[d], device_id_type=MESH)

    def first(q, carry):
        for i in range(3):
            total = inverse_ref[i, 0] * rhs_ref[q]
            total = total + inverse_ref[i, 1] * rhs_ref[loads + q]
            total = total + inverse_ref[i, 2] * rhs_ref[2 * loads + q]
            base[i * loads + q] = total
            x[0, i * loads + q, 8 : 8 + height, :] = total
        return carry

    lax.fori_loop(0, loads, first, 0)
    lane = lax.broadcasted_iota(jnp.int32, (height, LANES), 1)

    def pack(slot, step):
        sent[step, 0] = x[slot, :, 8, :]
        sent[step, 1] = x[slot, :, 7 + height, :]

        def columns(p, carry):
            left, right = carry
            plane = x[slot, p, 8 : 8 + height, :]
            left = jnp.where(lane == p, pltpu.roll(plane, p, 1), left)
            right = jnp.where(lane == p, pltpu.roll(plane, p + 1, 1), right)
            return left, right

        blank = jnp.zeros((height, LANES), jnp.float32)
        left, right = lax.fori_loop(0, planes, columns, (blank, blank), unroll=4)
        sent[step, 2, :height, :] = left
        sent[step, 3, :height, :] = right

    def copies(step, d):
        return pltpu.make_async_remote_copy(
            src_ref=sent.at[step, d],
            dst_ref=halo.at[step, d ^ 1],
            send_sem=send_sem.at[step, d],
            recv_sem=recv_sem.at[step, d ^ 1],
            device_id=peers[d],
            device_id_type=MESH,
        )

    def receives(step, d):
        return pltpu.make_async_remote_copy(
            src_ref=sent.at[step, d],
            dst_ref=halo.at[step, d],
            send_sem=send_sem.at[step, d],
            recv_sem=recv_sem.at[step, d],
            device_id=peers[d],
            device_id_type=MESH,
        )

    pack(0, 0)
    present = sum(e.astype(jnp.int32) for e in exists)
    pl.semaphore_wait(barrier, present)
    for step in range(ITERS - 1):
        old = step % 2
        for d in range(4):

            @pl.when(exists[d])
            def _():
                copies(step, d).start()

        if step == 0:

            def fold(d, carry):
                on = pattern_ref[d].astype(jnp.float32)
                for k in range(3):
                    column = [blocks_ref[d, j, k] * on for j in range(3)]
                    for i in range(3):
                        total = inverse_ref[i, 0] * column[0]
                        total = total + inverse_ref[i, 1] * column[1]
                        mixed[d, i, k] = total + inverse_ref[i, 2] * column[2]
                return carry

            lax.fori_loop(0, 4, fold, 0)
        for d in range(4):

            @pl.when(exists[d])
            def _():
                copies(step, d).wait_send()
                receives(step, d).wait_recv()

        x[old, :, 7, :] = halo[step, 0]
        x[old, :, 8 + height, :] = halo[step, 1]
        last = step == ITERS - 2

        def update(q, carry):
            totals = [base[i * loads + q] for i in range(3)]
            for k in range(3):
                p = k * loads + q
                plane = x[old, p, 8 : 8 + height, :]
                left = jnp.where(
                    lane == 0, pltpu.roll(halo[step, 2, :height, :], lax.rem(LANES - p, LANES), 1), pltpu.roll(plane, 1, 1)
                )
                right = jnp.where(
                    lane == LANES - 1,
                    pltpu.roll(halo[step, 3, :height, :], LANES - 1 - p, 1),
                    pltpu.roll(plane, LANES - 1, 1),
                )
                shifted = (x[old, p, 7 : 7 + height, :], x[old, p, 9 : 9 + height, :], left, right)
                for d in range(4):
                    for i in range(3):
                        totals[i] = totals[i] - mixed[d, i, k] * shifted[d]
            for i in range(3):
                if last:
                    out_ref[q, i] = totals[i]
                    planes_ref[i * loads + q] = totals[i]
                else:
                    x[1 - old, i * loads + q, 8 : 8 + height, :] = totals[i]
            return carry

        lax.fori_loop(0, loads, update, 0)
        if not last:
            pack(1 - old, step + 1)


def sweeps(rhs, inverse, blocks, pattern, row_count, col_count, loads):
    height = inverse.shape[2]
    planes = 3 * loads
    steps = ITERS - 1
    span = max(planes, height)
    return pl.pallas_call(
        functools.partial(sweep_kernel, row_count, col_count, loads),
        in_specs=[spec_vmem()] * 4,
        out_specs=(spec_vmem(), spec_vmem()),
        out_shape=(
            jax.ShapeDtypeStruct((loads, 3, height, LANES), jnp.float32),
            jax.ShapeDtypeStruct((planes, height, LANES), jnp.float32),
        ),
        scratch_shapes=[
            pltpu.VMEM((planes, height, LANES), jnp.float32),
            pltpu.VMEM((2, planes, height + 16, LANES), jnp.float32),
            pltpu.VMEM((4, 3, 3, height, LANES), jnp.float32),
            pltpu.VMEM((steps, 4, span, LANES), jnp.float32),
            pltpu.VMEM((steps, 4, span, LANES), jnp.float32),
            pltpu.SemaphoreType.DMA((steps, 4)),
            pltpu.SemaphoreType.DMA((steps, 4)),
        ],
        compiler_params=pltpu.CompilerParams(
            vmem_limit_bytes=VMEM_LIMIT, collective_id=0, has_side_effects=True
        ),
        name="sweeps",
    )(rhs.reshape(planes, height, LANES), inverse, blocks, pattern)


def prolong_kernel(devices, loads, chunk_ref, restriction_ref, pattern_ref, out_ref, values):
    groups = AGG_DEV // (LANES * GROUP)
    parts = LANES // devices
    rows = 3 * groups * parts

    @pl.when(pl.program_id(0) == 0)
    def _():
        for i in range(3):
            for group in range(groups):
                start = i * groups * parts + group * parts
                pieces = [chunk_ref[pl.ds(start + part, devices, stride=rows), :] for part in range(parts)]
                values[i, group] = jnp.concatenate(pieces, axis=0).T if parts > 1 else pieces[0].T

    for group in range(groups):
        for block in range(GROUP):
            b = group * GROUP + block
            lanes = slice(b * LANES, (b + 1) * LANES)
            present = pattern_ref[b : b + 1, :].astype(jnp.float32)
            terms = [values[i, group, block * loads : (block + 1) * loads, :] * present for i in range(3)]
            for j in range(3):
                total = restriction_ref[0, j : j + 1, lanes] * terms[0]
                total = total + restriction_ref[1, j : j + 1, lanes] * terms[1]
                out_ref[j, :, lanes] = total + restriction_ref[2, j : j + 1, lanes] * terms[2]


def prolong(chunks, restriction, pattern, devices, loads):
    pattern = pattern.reshape(-1, LANES)
    blocks = AGG_DEV // LANES
    groups = blocks // GROUP
    out = pl.pallas_call(
        functools.partial(prolong_kernel, devices, loads),
        grid=(FPA,),
        in_specs=[
            pl.BlockSpec(chunks.shape, lambda p: (0, 0)),
            pl.BlockSpec((3, 3, AGG_DEV), lambda p: (0, 0, p)),
            pl.BlockSpec((blocks, LANES), lambda p: (p, 0)),
        ],
        out_specs=pl.BlockSpec((3, loads, AGG_DEV), lambda p: (0, 0, p)),
        out_shape=jax.ShapeDtypeStruct((3, loads, restriction.shape[2]), jnp.float32),
        scratch_shapes=[pltpu.VMEM((3, groups, GROUP * loads, LANES), jnp.float32)],
        compiler_params=pltpu.CompilerParams(vmem_limit_bytes=VMEM_LIMIT),
        name="prolong",
    )(chunks, restriction, pattern)
    return out.transpose(1, 0, 2)


def exchange(chunks, devices):
    parts = chunks.reshape(devices, -1, LANES)
    parts = lax.all_to_all(parts, ("row", "col"), split_axis=0, concat_axis=0, tiled=True)
    return parts.reshape(-1, LANES)


def body(
    fine_residual,
    restriction,
    restriction_pattern,
    cell_aggregate,
    block_inverse,
    off_blocks,
    operator_pattern,
):
    loads = fine_residual.shape[0]
    row_count = lax.axis_size("row")
    col_count = lax.axis_size("col")
    devices = row_count * col_count
    height = cell_aggregate.shape[0]
    parts = LANES // devices
    piece = AGG_DEV // (LANES * GROUP) * parts
    owner = cell_aggregate // AGG_DEV
    order = cell_aggregate % AGG_DEV // devices
    cell_block = order // parts
    slots = (
        owner * (GROUP * piece)
        + cell_block % GROUP * piece
        + cell_block // GROUP * parts
        + order % parts
    ).reshape(-1)
    outgoing = restrict(fine_residual, restriction, restriction_pattern, devices)
    received = exchange(outgoing, devices)
    rhs = gather(slots, received, devices, loads, height)
    iterate, planes = sweeps(rhs, block_inverse, off_blocks, operator_pattern, row_count, col_count, loads)
    returning = scatter(slots, planes.reshape(-1, LANES), devices, loads)
    arrived = exchange(returning, devices)
    fine_correction = prolong(arrived, restriction, restriction_pattern, devices, loads)
    return (iterate, fine_correction)


def solution(mesh):
    in_specs = (
        P(None, None, ("row", "col")),
        P(None, None, ("row", "col")),
        P(("row", "col")),
        P("row", "col"),
        P(None, None, "row", "col"),
        P(None, None, None, "row", "col"),
        P(None, "row", "col"),
    )
    out_specs = (P(None, None, "row", "col"), P(None, None, ("row", "col")))
    return jax.shard_map(body, mesh=mesh, in_specs=in_specs, out_specs=out_specs, check_vma=False)
```

profile of v0, /device:TPU:1, one launch (start us, length us, event | category | flops | bytes accessed | tf_op | source)
XLA Modules:
  0.0 143.6 jit_solution(6690164984070134221)
XLA Ops:
  0.6 8.1 %restrict.1 = f32[2304,128]{1,0:T(8,128)} custom-call(f32[3,16,49152]{2,1,0:T(8,128)} %bitcast.11, f32[3,16,49152]{2,1,0:T(8,128)} %bitcast.12, f32[3,16,49152]{2,1,0:T(8,128)} %bitcast.13, f32[3,16,49152]{2,1,0:T(8,128)} %bitcast.14, f32[3,16,49152]{2,1,0:T(8,128)} %bitcast.15, f32[3,16,49152]{2,1,0:T(8,128)} %bitcast.16, f32[3,16,49152]{2,1,0:T(8,128)} %bitcast.17, ...), custom_call_target="tpu_custom_call" | custom-call | tf_op jit(solution)/shard_map/restrict/pallas_call | solution.py:62
  8.7 0.0 copy-start.3
  8.7 7.1 %all-to-all-start = ((f32[32,72,128]{2,1,0:T(8,128)}), f32[32,72,128]{2,1,0:T(8,128)S(1)}, u32[]{:S(2)}, u32[]{:S(2)}) async-start(f32[32,72,128]{2,1,0:T(8,128)} %bitcast.33), calls=%async_computation | async-start | bytes 2359296 | tf_op jit(solution)/shard_map/all_to_all | solution.py:386
  15.8 0.0 copy-done.3
  15.8 0.7 fusion.4.slots_ref
  16.5 27.9 %all-to-all-done = f32[32,72,128]{2,1,0:T(8,128)S(1)} async-done(((f32[32,72,128]{2,1,0:T(8,128)}), f32[32,72,128]{2,1,0:T(8,128)S(1)}, u32[]{:S(2)}, u32[]{:S(2)}) %all-to-all-start) | async-done | bytes 1179680 | tf_op jit(solution)/shard_map/all_to_all | solution.py:386
  44.4 0.0 copy-start.1
  44.4 1.0 copy-done.1
  45.4 15.1 %gather_cells.1 = f32[2304,128]{1,0:T(8,128)} custom-call(s32[6144]{0:T(1024)} %fusion.4.slots_ref, f32[2304,128]{1,0:T(8,128)} %bitcast.30), custom_call_target="tpu_custom_call" | custom-call | tf_op jit(solution)/shard_map/gather_cells/pallas_call | solution.py:105
  60.5 25.0 %sweeps.1 = (f32[16,3,48,128]{3,2,1,0:T(8,128)}, f32[48,48,128]{2,1,0:T(8,128)}) custom-call(f32[48,48,128]{2,1,0:T(8,128)} %bitcast.32, f32[3,3,48,128]{3,2,1,0:T(8,128)} %inverse_ref.1, f32[4,3,3,48,128]{4,3,2,1,0:T(8,128)} %blocks_ref.1, s32[4,48,128]{2,1,0:T(8,128)} %pattern_ref.1), custom_call_target="tpu_custom_call" | custom-call | tf_op jit(solution)/shard_map/sweeps/pallas_call | solution.py:314
  85.6 14.8 %scatter_cells.1 = f32[2304,128]{1,0:T(8,128)} custom-call(s32[6144]{0:T(1024)} %fusion.4.slots_ref, f32[2304,128]{1,0:T(8,128)} %bitcast.34), custom_call_target="tpu_custom_call" | custom-call | tf_op jit(solution)/shard_map/scatter_cells/pallas_call | solution.py:148
  100.4 4.0 %all-to-all-start.1 = ((f32[32,72,128]{2,1,0:T(8,128)}), f32[32,72,128]{2,1,0:T(8,128)S(1)}, u32[]{:S(2)}, u32[]{:S(2)}) async-start(f32[32,72,128]{2,1,0:T(8,128)} %bitcast.31), calls=%async_computation.1 | async-start | bytes 2359296 | tf_op jit(solution)/shard_map/all_to_all | solution.py:386
  104.4 28.6 %all-to-all-done.1 = f32[32,72,128]{2,1,0:T(8,128)S(1)} async-done(((f32[32,72,128]{2,1,0:T(8,128)}), f32[32,72,128]{2,1,0:T(8,128)S(1)}, u32[]{:S(2)}, u32[]{:S(2)}) %all-to-all-start.1) | async-done | bytes 1179680 | tf_op jit(solution)/shard_map/all_to_all | solution.py:386
  133.0 0.0 copy-start
  133.0 1.0 copy-done
  134.0 0.0 copy-start.2
  134.0 8.5 %prolong.1 = f32[3,16,49152]{2,1,0:T(8,128)} custom-call(f32[2304,128]{1,0:T(8,128)} %bitcast.29, f32[3,3,49152]{2,1,0:T(4,128)} %restriction_ref.1, s32[384,128]{1,0:T(8,128)} %bitcast.27), custom_call_target="tpu_custom_call" | custom-call | tf_op jit(solution)/shard_map/prolong/pallas_call | solution.py:367
  142.6 0.0 copy-done.2
  142.6 1.0 copy.10
Async XLA Ops:
  8.7 7.1 %copy-start.3 = (s32[48,128]{1,0:T(8,128)S(1)}, s32[48,128]{1,0:T(8,128)}, u32[]{:S(2)}) copy-start(s32[48,128]{1,0:T(8,128)} %param.10) | copy-start | bytes 73732
  8.7 35.7 %all-to-all-start = ((f32[32,72,128]{2,1,0:T(8,128)}), f32[32,72,128]{2,1,0:T(8,128)S(1)}, u32[]{:S(2)}, u32[]{:S(2)}) async-start(f32[32,72,128]{2,1,0:T(8,128)} %bitcast.33), calls=%async_computation | async-start | bytes 2359296 | tf_op jit(solution)/shard_map/all_to_all | solution.py:386
  44.4 1.0 copy-start.1
  100.4 32.6 %all-to-all-start.1 = ((f32[32,72,128]{2,1,0:T(8,128)}), f32[32,72,128]{2,1,0:T(8,128)S(1)}, u32[]{:S(2)}, u32[]{:S(2)}) async-start(f32[32,72,128]{2,1,0:T(8,128)} %bitcast.31), calls=%async_computation.1 | async-start | bytes 2359296 | tf_op jit(solution)/shard_map/all_to_all | solution.py:386
  133.0 1.0 copy-start
  134.0 8.5 %copy-start.2 = (f32[16,3,48,128]{3,2,1,0:T(8,128)S(1)}, f32[16,3,48,128]{3,2,1,0:T(8,128)}, u32[]{:S(2)}) copy-start(f32[16,3,48,128]{3,2,1,0:T(8,128)} %get-tuple-element.8) | copy-start | bytes 3538948
where the time goes:
time: 145 us; the launch traced here: 144 us
  Pallas kernels  71.6 us (49%)
  waiting for transfers between devices  56.5 us (39%)
  starting transfers between devices  11.1 us (8%)
  local copies, waits for them, and re-layouts  3.05 us (2%)
    all_to_all x2, waiting for transfers between devices, exchange(): lax.all_to_all(parts, ('row', 'col'), split_axis=0, concat_axis=0, tiled=...  56.5 us
    pallas_call x1, Pallas kernels, sweeps(): pl.pallas_call(functools.partial(sweep_kernel, row_count, col_count, load...  25 us
    pallas_call x1, Pallas kernels, gather(): pl.pallas_call(functools.partial(gather_kernel, devices, loads), in_specs...  15.1 us
    pallas_call x1, Pallas kernels, scatter(): pl.pallas_call(functools.partial(scatter_kernel, devices, loads), in_spec...  14.8 us
    all_to_all x2, starting transfers between devices, exchange(): lax.all_to_all(parts, ('row', 'col'), split_axis=0, concat_axis=0, tiled=...  11.1 us
    pallas_call x1, Pallas kernels, prolong(): pl.pallas_call(functools.partial(prolong_kernel, devices, loads), grid=(F...  8.53 us
    pallas_call x1, Pallas kernels, restrict(): pl.pallas_call(functools.partial(restrict_kernel, devices, loads), grid=(...  8.08 us
    unnamed x9, local copies, waits for them, and re-layouts  3.05 us
  transfers between devices with their start and end apart: 2, of which 2 were waited for; matrix products, arithmetic and copies ran while one was open for 0% of the time, Pallas kernels for 0%

commit v1 on v0

--- a/solution.py
+++ b/solution.py
@@ -12,6 +12,7 @@
 AGG_DEV = 6144
 LANES = 128
 GROUP = 8
+PAIR = 2
 MESH = pl.DeviceIdType.MESH
 VMEM_LIMIT = 56 * 1024 * 1024
 
@@ -20,85 +21,160 @@
     return pl.BlockSpec(memory_space=pltpu.VMEM)
 
 
-def restrict_kernel(devices, loads, *refs):
+def peer_of(me, index, devices, col_count):
+    peer = lax.rem(me + 13 * index, devices)
+    return peer, {"row": peer // col_count, "col": lax.rem(peer, col_count)}
+
+
+def greet(devices, col_count, me):
+    barrier = pltpu.get_barrier_semaphore()
+
+    def signal(index, carry):
+        _, where = peer_of(me, index, devices, col_count)
+        pl.semaphore_signal(barrier, inc=1, device_id=where, device_id_type=MESH)
+        return carry
+
+    lax.fori_loop(1, devices, signal, 0)
+    return barrier
+
+
+def restrict_kernel(devices, col_count, loads, *refs):
     residuals = refs[0:FPA]
     restrictions = refs[FPA : 2 * FPA]
     patterns = refs[2 * FPA : 3 * FPA]
-    out_ref = refs[3 * FPA]
-    stage = refs[3 * FPA + 1]
-    group = pl.program_id(0)
-    groups = AGG_DEV // (LANES * GROUP)
+    out_ref, stage, sent, send_sem, recv_sem, own_sem = refs[3 * FPA :]
+    pair = pl.program_id(0)
+    pairs = pl.num_programs(0)
     parts = LANES // devices
-    rows = 3 * groups * parts
-    for block in range(GROUP):
-        lanes = slice(block * LANES, (block + 1) * LANES)
-        totals = [None, None, None]
-        for p in range(FPA):
-            present = patterns[p][block : block + 1, :].astype(jnp.float32)
-            for j in range(3):
-                masked = residuals[p][j, :, lanes] * present
-                for i in range(3):
-                    term = restrictions[p][i, j : j + 1, lanes] * masked
-                    totals[i] = term if totals[i] is None else totals[i] + term
+    me = lax.axis_index("row") * col_count + lax.axis_index("col")
+    barrier = pltpu.get_barrier_semaphore()
+
+    @pl.when(pair == 0)
+    def _():
+        greet(devices, col_count, me)
+
+    for half in range(PAIR):
+        for block in range(GROUP):
+            start = (half * GROUP + block) * LANES
+            lanes = slice(start, start + LANES)
+            totals = [None, None, None]
+            for p in range(FPA):
+                present = patterns[p][0, half * GROUP + block : half * GROUP + block + 1, :].astype(jnp.float32)
+                for j in range(3):
+                    masked = residuals[p][j, :, lanes] * present
+                    for i in range(3):
+                        term = restrictions[p][i, j : j + 1, lanes] * masked
+                        totals[i] = term if totals[i] is None else totals[i] + term
+            for i in range(3):
+                stage[i, block * loads : (block + 1) * loads, :] = totals[i]
         for i in range(3):
-            stage[i, block * loads : (block + 1) * loads, :] = totals[i]
-    for i in range(3):
-        turned = stage[i].T
-        for part in range(parts):
-            start = i * groups * parts + group * parts + part
-            out_ref[pl.ds(start, devices, stride=rows), :] = turned[part * devices : (part + 1) * devices, :]
-
-
-def restrict(residual, restriction, pattern, devices):
+            turned = stage[i].T
+            for part in range(parts):
+                sent[pair, :, (i * PAIR + half) * parts + part, :] = turned[part * devices : (part + 1) * devices, :]
+
+    @pl.when(pair == 0)
+    def _():
+        pl.semaphore_wait(barrier, devices - 1)
+
+    def send(index, carry):
+        peer, where = peer_of(me, index, devices, col_count)
+        pltpu.make_async_remote_copy(
+            src_ref=sent.at[pair, peer],
+            dst_ref=out_ref.at[pair, me],
+            send_sem=send_sem,
+            recv_sem=recv_sem,
+            device_id=where,
+            device_id_type=MESH,
+        ).start()
+        return carry
+
+    lax.fori_loop(1, devices, send, 0)
+
+    @pl.when(pair == pairs - 1)
+    def _():
+        own = pltpu.make_async_copy(sent.at[:, me], out_ref.at[:, me], own_sem)
+        own.start()
+        own.wait()
+        _, where = peer_of(me, 1, devices, col_count)
+        every = pltpu.make_async_remote_copy(
+            src_ref=sent.at[:, pl.ds(0, devices - 1)],
+            dst_ref=out_ref.at[:, pl.ds(0, devices - 1)],
+            send_sem=send_sem,
+            recv_sem=recv_sem,
+            device_id=where,
+            device_id_type=MESH,
+        )
+        every.wait_send()
+        every.wait_recv()
+
+
+def restrict(residual, restriction, pattern, devices, col_count):
     loads = residual.shape[0]
     residual = residual.transpose(1, 0, 2)
-    pattern = pattern.reshape(-1, LANES)
-    width = LANES * GROUP
-    groups = AGG_DEV // width
-    rows = 3 * groups * (LANES // devices)
-    res_specs = [pl.BlockSpec((3, loads, width), functools.partial(lambda p, g: (0, 0, p * groups + g), p)) for p in range(FPA)]
-    rst_specs = [pl.BlockSpec((3, 3, width), functools.partial(lambda p, g: (0, 0, p * groups + g), p)) for p in range(FPA)]
-    pat_specs = [pl.BlockSpec((GROUP, LANES), functools.partial(lambda p, g: (p * groups + g, 0), p)) for p in range(FPA)]
+    width = LANES * GROUP * PAIR
+    pairs = AGG_DEV // width
+    pattern = pattern.reshape(-1, GROUP * PAIR, LANES)
+    rows = 3 * PAIR * (LANES // devices)
+    res_specs = [pl.BlockSpec((3, loads, width), functools.partial(lambda p, g: (0, 0, p * pairs + g), p)) for p in range(FPA)]
+    rst_specs = [pl.BlockSpec((3, 3, width), functools.partial(lambda p, g: (0, 0, p * pairs + g), p)) for p in range(FPA)]
+    pat_specs = [pl.BlockSpec((1, GROUP * PAIR, LANES), functools.partial(lambda p, g: (p * pairs + g, 0, 0), p)) for p in range(FPA)]
     return pl.pallas_call(
-        functools.partial(restrict_kernel, devices, loads),
-        grid=(groups,),
+        functools.partial(restrict_kernel, devices, col_count, loads),
+        grid=(pairs,),
         in_specs=res_specs + rst_specs + pat_specs,
-        out_specs=pl.BlockSpec((devices * rows, LANES), lambda g: (0, 0)),
-        out_shape=jax.ShapeDtypeStruct((devices * rows, LANES), jnp.float32),
-        scratch_shapes=[pltpu.VMEM((3, LANES, LANES), jnp.float32)],
-        compiler_params=pltpu.CompilerParams(vmem_limit_bytes=VMEM_LIMIT),
-        name="restrict",
+        out_specs=pl.BlockSpec(memory_space=pl.ANY),
+        out_shape=jax.ShapeDtypeStruct((pairs, devices, rows, LANES), jnp.float32),
+        scratch_shapes=[
+            pltpu.VMEM((3, LANES, LANES), jnp.float32),
+            pltpu.VMEM((pairs, devices, rows, LANES), jnp.float32),
+            pltpu.SemaphoreType.DMA,
+            pltpu.SemaphoreType.DMA,
+            pltpu.SemaphoreType.DMA,
+        ],
+        compiler_params=pltpu.CompilerParams(
+            vmem_limit_bytes=VMEM_LIMIT,
+            collective_id=1,
+            has_side_effects=True,
+            dimension_semantics=("arbitrary",),
+        ),
+        name="restrict_send",
     )(*([residual] * FPA + [restriction] * FPA + [pattern] * FPA))
 
 
-def gather_kernel(devices, loads, slots_ref, chunk_ref, out_ref, table, staged):
-    groups = AGG_DEV // (LANES * GROUP)
-    piece = groups * (LANES // devices)
-    lane = lax.broadcasted_iota(jnp.int32, (piece, LANES), 1)
+def gather_kernel(devices, loads, slots_ref, chunk_ref, out_ref, table, ordered):
+    pairs = chunk_ref.shape[0]
+    few = PAIR * (LANES // devices)
+    piece = pairs * few
+    lane = lax.broadcasted_iota(jnp.int32, (few, LANES), 1)
 
     def unpack(f, carry):
-        base = f * (3 * piece)
-        parts = [chunk_ref[pl.ds(base + i * piece, piece), :] for i in range(3)]
-        for block in range(GROUP):
-            moved = []
-            for i in range(3):
-                shift = ((i - block) * loads) % LANES
-                moved.append(pltpu.roll(parts[i], shift, 1) if shift else parts[i])
-            row = jnp.where(lane < loads, moved[0], jnp.where(lane < 2 * loads, moved[1], moved[2]))
-            table[pl.ds(f * (GROUP * piece) + block * piece, piece), :] = row
-        return carry
-
-    lax.fori_loop(0, devices, unpack, 0)
+        for pair in range(pairs):
+            parts = [chunk_ref[pair, f, i * few : (i + 1) * few, :] for i in range(3)]
+            for block in range(GROUP):
+                moved = []
+                for i in range(3):
+                    shift = ((i - block) * loads) % LANES
+                    moved.append(pltpu.roll(parts[i], shift, 1) if shift else parts[i])
+                row = jnp.where(lane < loads, moved[0], jnp.where(lane < 2 * loads, moved[1], moved[2]))
+                table[pl.ds(f * (GROUP * piece) + block * piece + pair * few, few), :] = row
+        return carry
+
+    lax.fori_loop(0, devices, unpack, 0, unroll=2)
     height = out_ref.shape[0] // (3 * loads)
 
     def take(r, carry):
         for c in range(LANES):
-            staged[pl.ds(c, 1), :] = table[pl.ds(slots_ref[r * LANES + c], 1), :]
-        turned = staged[...].T
+            ordered[pl.ds(r * LANES + c, 1), :] = table[pl.ds(slots_ref[r * LANES + c], 1), :]
+        return carry
+
+    lax.fori_loop(0, height, take, 0)
+
+    def turn(r, carry):
+        turned = ordered[pl.ds(pl.multiple_of(r * LANES, LANES), LANES), :].T
         out_ref[pl.ds(r, 3 * loads, stride=height), :] = turned[: 3 * loads, :]
         return carry
 
-    lax.fori_loop(0, height, take, 0)
+    lax.fori_loop(0, height, turn, 0, unroll=4)
 
 
 def gather(slots, chunks, devices, loads, height):
@@ -107,28 +183,50 @@
         in_specs=[pl.BlockSpec(memory_space=pltpu.SMEM), spec_vmem()],
         out_specs=spec_vmem(),
         out_shape=jax.ShapeDtypeStruct((3 * loads * height, LANES), jnp.float32),
-        scratch_shapes=[pltpu.VMEM((AGG_DEV, LANES), jnp.float32), pltpu.VMEM((LANES, LANES), jnp.float32)],
+        scratch_shapes=[pltpu.VMEM((AGG_DEV, LANES), jnp.float32), pltpu.VMEM((height * LANES, LANES), jnp.float32)],
         compiler_params=pltpu.CompilerParams(vmem_limit_bytes=VMEM_LIMIT),
         name="gather_cells",
     )(slots, chunks)
 
 
-def scatter_kernel(devices, loads, slots_ref, solution_ref, out_ref, table, staged):
-    groups = AGG_DEV // (LANES * GROUP)
-    piece = groups * (LANES // devices)
+def scatter_kernel(loads, slots_ref, solution_ref, table, ordered):
     height = solution_ref.shape[0] // (3 * loads)
-    staged[...] = jnp.zeros_like(staged)
+
+    def turn(r, carry):
+        plane = solution_ref[pl.ds(r, 3 * loads, stride=height), :]
+        ordered[pl.ds(pl.multiple_of(r * LANES, LANES), LANES), : 3 * loads] = plane.T
+        return carry
+
+    lax.fori_loop(0, height, turn, 0, unroll=4)
 
     def put(r, carry):
-        staged[:, : 3 * loads] = solution_ref[pl.ds(r, 3 * loads, stride=height), :].T
         for c in range(LANES):
-            table[pl.ds(slots_ref[r * LANES + c], 1), :] = staged[pl.ds(c, 1), :]
+            table[pl.ds(slots_ref[r * LANES + c], 1), :] = ordered[pl.ds(r * LANES + c, 1), :]
         return carry
 
     lax.fori_loop(0, height, put, 0)
+
+
+def scatter(slots, solution_planes, loads):
+    height = solution_planes.shape[0] // (3 * loads)
+    return pl.pallas_call(
+        functools.partial(scatter_kernel, loads),
+        in_specs=[pl.BlockSpec(memory_space=pltpu.SMEM), spec_vmem()],
+        out_specs=spec_vmem(),
+        out_shape=jax.ShapeDtypeStruct((AGG_DEV, LANES), jnp.float32),
+        scratch_shapes=[pltpu.VMEM((height * LANES, LANES), jnp.float32)],
+        compiler_params=pltpu.CompilerParams(vmem_limit_bytes=VMEM_LIMIT),
+        name="scatter_cells",
+    )(slots, solution_planes)
+
+
+def pack_kernel(devices, col_count, loads, table, out_ref, sent, send_sem, recv_sem, own_sem):
+    piece = AGG_DEV // (GROUP * devices)
+    me = lax.axis_index("row") * col_count + lax.axis_index("col")
+    barrier = greet(devices, col_count, me)
     lane = lax.broadcasted_iota(jnp.int32, (piece, LANES), 1)
 
-    def pack(f, carry):
+    def pack(f):
         rows = [table[pl.ds(f * (GROUP * piece) + block * piece, piece), :] for block in range(GROUP)]
         for i in range(3):
             total = None
@@ -136,24 +234,57 @@
                 shift = ((block - i) * loads) % LANES
                 moved = pltpu.roll(rows[block], shift, 1) if shift else rows[block]
                 total = moved if total is None else jnp.where(lane < block * loads, total, moved)
-            out_ref[pl.ds(f * (3 * piece) + i * piece, piece), :] = total
-        return carry
-
-    lax.fori_loop(0, devices, pack, 0)
-
-
-def scatter(slots, solution_planes, devices, loads):
-    groups = AGG_DEV // (LANES * GROUP)
-    piece = groups * (LANES // devices)
+            sent[f, i * piece : (i + 1) * piece, :] = total
+
+    pack(me)
+    own = pltpu.make_async_copy(sent.at[me], out_ref.at[me], own_sem)
+    own.start()
+    pl.semaphore_wait(barrier, devices - 1)
+
+    def send(index, carry):
+        peer, where = peer_of(me, index, devices, col_count)
+        pack(peer)
+        pltpu.make_async_remote_copy(
+            src_ref=sent.at[peer],
+            dst_ref=out_ref.at[me],
+            send_sem=send_sem,
+            recv_sem=recv_sem,
+            device_id=where,
+            device_id_type=MESH,
+        ).start()
+        return carry
+
+    lax.fori_loop(1, devices, send, 0)
+    own.wait()
+    _, where = peer_of(me, 1, devices, col_count)
+    every = pltpu.make_async_remote_copy(
+        src_ref=sent.at[pl.ds(0, devices - 1)],
+        dst_ref=out_ref.at[pl.ds(0, devices - 1)],
+        send_sem=send_sem,
+        recv_sem=recv_sem,
+        device_id=where,
+        device_id_type=MESH,
+    )
+    every.wait_send()
+    every.wait_recv()
+
+
+def pack_send(table, devices, col_count, loads):
+    piece = AGG_DEV // (GROUP * devices)
     return pl.pallas_call(
-        functools.partial(scatter_kernel, devices, loads),
-        in_specs=[pl.BlockSpec(memory_space=pltpu.SMEM), spec_vmem()],
-        out_specs=spec_vmem(),
-        out_shape=jax.ShapeDtypeStruct((devices * 3 * piece, LANES), jnp.float32),
-        scratch_shapes=[pltpu.VMEM((AGG_DEV, LANES), jnp.float32), pltpu.VMEM((LANES, LANES), jnp.float32)],
-        compiler_params=pltpu.CompilerParams(vmem_limit_bytes=VMEM_LIMIT),
-        name="scatter_cells",
-    )(slots, solution_planes)
+        functools.partial(pack_kernel, devices, col_count, loads),
+        in_specs=[spec_vmem()],
+        out_specs=pl.BlockSpec(memory_space=pl.ANY),
+        out_shape=jax.ShapeDtypeStruct((devices, 3 * piece, LANES), jnp.float32),
+        scratch_shapes=[
+            pltpu.VMEM((devices, 3 * piece, LANES), jnp.float32),
+            pltpu.SemaphoreType.DMA,
+            pltpu.SemaphoreType.DMA,
+            pltpu.SemaphoreType.DMA,
+        ],
+        compiler_params=pltpu.CompilerParams(vmem_limit_bytes=VMEM_LIMIT, collective_id=2, has_side_effects=True),
+        name="pack_send",
+    )(table)
 
 
 def sweep_kernel(
@@ -381,12 +512,6 @@
     return out.transpose(1, 0, 2)
 
 
-def exchange(chunks, devices):
-    parts = chunks.reshape(devices, -1, LANES)
-    parts = lax.all_to_all(parts, ("row", "col"), split_axis=0, concat_axis=0, tiled=True)
-    return parts.reshape(-1, LANES)
-
-
 def body(
     fine_residual,
     restriction,
@@ -412,12 +537,11 @@
         + cell_block // GROUP * parts
         + order % parts
     ).reshape(-1)
-    outgoing = restrict(fine_residual, restriction, restriction_pattern, devices)
-    received = exchange(outgoing, devices)
+    received = restrict(fine_residual, restriction, restriction_pattern, devices, col_count)
     rhs = gather(slots, received, devices, loads, height)
     iterate, planes = sweeps(rhs, block_inverse, off_blocks, operator_pattern, row_count, col_count, loads)
-    returning = scatter(slots, planes.reshape(-1, LANES), devices, loads)
-    arrived = exchange(returning, devices)
+    table = scatter(slots, planes.reshape(-1, LANES), loads)
+    arrived = pack_send(table, devices, col_count, loads).reshape(-1, LANES)
     fine_correction = prolong(arrived, restriction, restriction_pattern, devices, loads)
     return (iterate, fine_correction)
 

time: 145 us -> 129 us (0.89)
  waiting for transfers between devices: 56.5 us -> 0 us
  Pallas kernels: 71.6 us -> 125 us
  starting transfers between devices: 11.1 us -> 0 us
  local copies, waits for them, and re-layouts: 3.05 us -> 1.02 us
    pallas_call x2 -> x3, Pallas kernels: 22.9 us -> 80.3 us  [the longest x1 35.6 us: restrict(): pl.pallas_call(functools.partial(restrict_kernel, devices, col_count, loa...]
    all_to_all x2 -> x0, waiting for transfers between devices: 56.5 us -> none  [exchange(): lax.all_to_all(parts, ('row', 'col'), split_axis=0, concat_axis=0, tiled=...]
    all_to_all x2 -> x0, starting transfers between devices: 11.1 us -> none  [exchange(): lax.all_to_all(parts, ('row', 'col'), split_axis=0, concat_axis=0, tiled=...]
    pallas_call x1, Pallas kernels: 15.1 us -> 12 us  [gather(): pl.pallas_call(functools.partial(gather_kernel, devices, loads), in_specs...]
    unnamed x9 -> x3, local copies, waits for them, and re-layouts: 3.05 us -> 1.02 us
  transfers between devices with their start and end apart: 2 -> 0, of which waited for: 2 -> 0; matrix products, arithmetic and copies ran while one was open for 0% -> 0% of each run, Pallas kernels for 0% -> 0%
where the time goes in v1:
time: 129 us; the launch traced here: 128 us
  Pallas kernels  125 us (97%)
  other arithmetic  1.43 us (1%)
    pallas_call x1, Pallas kernels, restrict(): pl.pallas_call(functools.partial(restrict_kernel, devices, col_count, loa...  35.6 us
    pallas_call x1, Pallas kernels, pack_send(): pl.pallas_call(functools.partial(pack_kernel, devices, col_count, loads),...  35.1 us
    pallas_call x1, Pallas kernels, sweeps(): pl.pallas_call(functools.partial(sweep_kernel, row_count, col_count, load...  24.3 us
    pallas_call x1, Pallas kernels, gather(): pl.pallas_call(functools.partial(gather_kernel, devices, loads), in_specs...  12 us
    pallas_call x1, Pallas kernels, scatter(): pl.pallas_call(functools.partial(scatter_kernel, loads), in_specs=[pl.Blo...  9.67 us
    pallas_call x1, Pallas kernels, prolong(): pl.pallas_call(functools.partial(prolong_kernel, devices, loads), grid=(F...  8.54 us

profile of v1, /device:TPU:1, one launch (start us, length us, event | category | flops | bytes accessed | tf_op | source)
XLA Modules:
  0.0 128.3 jit_solution(17885896964117434462)
XLA Ops:
  0.6 1.4 %fusion.4.slots_ref = s32[6144]{0:T(1024)} fusion(s32[48,128]{1,0:T(8,128)} %param.10), kind=kLoop, calls=%fused_computation.20 | loop fusion | flops 436224 | bytes 49152 | tf_op jit(solution)/shard_map/reshape | solution.py:539
  2.1 35.6 %restrict_send.1.chunk_ref = f32[3,32,24,128]{3,2,1,0:T(8,128)} custom-call(f32[3,16,49152]{2,1,0:T(8,128)} %bitcast.9, f32[3,16,49152]{2,1,0:T(8,128)} %bitcast.10, f32[3,16,49152]{2,1,0:T(8,128)} %bitcast.11, f32[3,16,49152]{2,1,0:T(8,128)} %bitcast.12, f32[3,16,49152]{2,1,0:T(8,128)} %bitcast.13, f32[3,16,49152]{2,1,0:T(8,128)} %bitcast.14, ...), custom_call_target="tpu_custom_call" | custom-call | tf_op jit(solution)/shard_map/restrict_send/pallas_call | solution.py:121
  37.6 12.0 %gather_cells.1 = f32[2304,128]{1,0:T(8,128)} custom-call(s32[6144]{0:T(1024)} %fusion.4.slots_ref, f32[3,32,24,128]{3,2,1,0:T(8,128)} %restrict_send.1.chunk_ref), custom_call_target="tpu_custom_call" | custom-call | tf_op jit(solution)/shard_map/gather_cells/pallas_call | solution.py:181
  49.6 24.3 %sweeps.1 = (f32[16,3,48,128]{3,2,1,0:T(8,128)}, f32[48,48,128]{2,1,0:T(8,128)}) custom-call(f32[48,48,128]{2,1,0:T(8,128)} %bitcast.28, f32[3,3,48,128]{3,2,1,0:T(8,128)} %inverse_ref.1, f32[4,3,3,48,128]{4,3,2,1,0:T(8,128)} %blocks_ref.1, s32[4,48,128]{2,1,0:T(8,128)} %pattern_ref.1), custom_call_target="tpu_custom_call" | custom-call | tf_op jit(solution)/shard_map/sweeps/pallas_call | solution.py:445
  73.9 9.7 %scatter_cells.1.table = f32[6144,128]{1,0:T(8,128)} custom-call(s32[6144]{0:T(1024)} %fusion.4.slots_ref, f32[2304,128]{1,0:T(8,128)} %bitcast.29), custom_call_target="tpu_custom_call" | custom-call | tf_op jit(solution)/shard_map/scatter_cells/pallas_call | solution.py:212
  83.6 35.1 %pack_send.1 = f32[32,72,128]{2,1,0:T(8,128)} custom-call(f32[6144,128]{1,0:T(8,128)} %scatter_cells.1.table), custom_call_target="tpu_custom_call" | custom-call | tf_op jit(solution)/shard_map/pack_send/pallas_call | solution.py:274
  118.7 0.0 copy-start
  118.7 8.5 %prolong.1 = f32[3,16,49152]{2,1,0:T(8,128)} custom-call(f32[2304,128]{1,0:T(8,128)} %bitcast.27, f32[3,3,49152]{2,1,0:T(4,128)} %restriction_ref.1, s32[384,128]{1,0:T(8,128)} %bitcast.25), custom_call_target="tpu_custom_call" | custom-call | tf_op jit(solution)/shard_map/prolong/pallas_call | solution.py:498
  127.2 0.0 copy-done
  127.2 1.0 copy.10
Async XLA Ops:
  118.7 8.6 %copy-start = (f32[16,3,48,128]{3,2,1,0:T(8,128)S(1)}, f32[16,3,48,128]{3,2,1,0:T(8,128)}, u32[]{:S(2)}) copy-start(f32[16,3,48,128]{3,2,1,0:T(8,128)} %get-tuple-element.8) | copy-start | bytes 3538948

commit v2 on v1

--- a/solution.py
+++ b/solution.py
@@ -13,6 +13,7 @@
 LANES = 128
 GROUP = 8
 PAIR = 2
+HALVES = 2
 MESH = pl.DeviceIdType.MESH
 VMEM_LIMIT = 56 * 1024 * 1024
 
@@ -189,7 +190,7 @@
     )(slots, chunks)
 
 
-def scatter_kernel(loads, slots_ref, solution_ref, table, ordered):
+def scatter_kernel(loads, slots_ref, solution_ref, table, out_ref, ordered):
     height = solution_ref.shape[0] // (3 * loads)
 
     def turn(r, carry):
@@ -205,6 +206,14 @@
         return carry
 
     lax.fori_loop(0, height, put, 0)
+
+    def write(q, carry):
+        for i in range(3):
+            start = pl.multiple_of((i * loads + q) * height, height)
+            out_ref[q, i] = solution_ref[pl.ds(start, height), :]
+        return carry
+
+    lax.fori_loop(0, loads, write, 0)
 
 
 def scatter(slots, solution_planes, loads):
@@ -212,8 +221,11 @@
     return pl.pallas_call(
         functools.partial(scatter_kernel, loads),
         in_specs=[pl.BlockSpec(memory_space=pltpu.SMEM), spec_vmem()],
-        out_specs=spec_vmem(),
-        out_shape=jax.ShapeDtypeStruct((AGG_DEV, LANES), jnp.float32),
+        out_specs=(spec_vmem(), spec_vmem()),
+        out_shape=(
+            jax.ShapeDtypeStruct((AGG_DEV, LANES), jnp.float32),
+            jax.ShapeDtypeStruct((loads, 3, height, LANES), jnp.float32),
+        ),
         scratch_shapes=[pltpu.VMEM((height * LANES, LANES), jnp.float32)],
         compiler_params=pltpu.CompilerParams(vmem_limit_bytes=VMEM_LIMIT),
         name="scatter_cells",
@@ -241,9 +253,8 @@
     own.start()
     pl.semaphore_wait(barrier, devices - 1)
 
-    def send(index, carry):
+    def send(index):
         peer, where = peer_of(me, index, devices, col_count)
-        pack(peer)
         pltpu.make_async_remote_copy(
             src_ref=sent.at[peer],
             dst_ref=out_ref.at[me],
@@ -252,9 +263,15 @@
             device_id=where,
             device_id_type=MESH,
         ).start()
-        return carry
-
-    lax.fori_loop(1, devices, send, 0)
+
+    def step(index, carry):
+        pack(peer_of(me, index, devices, col_count)[0])
+        send(index - 1)
+        return carry
+
+    pack(peer_of(me, 1, devices, col_count)[0])
+    lax.fori_loop(2, devices, step, 0)
+    send(devices - 1)
     own.wait()
     _, where = peer_of(me, 1, devices, col_count)
     every = pltpu.make_async_remote_copy(
@@ -295,7 +312,6 @@
     inverse_ref,
     blocks_ref,
     pattern_ref,
-    out_ref,
     planes_ref,
     base,
     x,
@@ -306,7 +322,8 @@
     recv_sem,
 ):
     height = inverse_ref.shape[2]
-    planes = 3 * loads
+    few = loads // HALVES
+    planes = 3 * few
     row = lax.axis_index("row")
     col = lax.axis_index("col")
     exists = (row > 0, row < row_count - 1, col > 0, col < col_count - 1)
@@ -316,6 +333,7 @@
         {"row": row, "col": col - 1},
         {"row": row, "col": col + 1},
     )
+    extent = (planes, planes, height, height)
     barrier = pltpu.get_barrier_semaphore()
     halo[...] = jnp.zeros_like(halo)
     for d in range(4):
@@ -324,140 +342,141 @@
         def _():
             pl.semaphore_signal(barrier, inc=1, device_id=peers[d], device_id_type=MESH)
 
-    def first(q, carry):
-        for i in range(3):
-            total = inverse_ref[i, 0] * rhs_ref[q]
-            total = total + inverse_ref[i, 1] * rhs_ref[loads + q]
-            total = total + inverse_ref[i, 2] * rhs_ref[2 * loads + q]
-            base[i * loads + q] = total
-            x[0, i * loads + q, 8 : 8 + height, :] = total
-        return carry
-
-    lax.fori_loop(0, loads, first, 0)
     lane = lax.broadcasted_iota(jnp.int32, (height, LANES), 1)
 
-    def pack(slot, step):
-        sent[step, 0] = x[slot, :, 8, :]
-        sent[step, 1] = x[slot, :, 7 + height, :]
+    def first(half):
+        def one(q, carry):
+            source = half * few + q
+            for i in range(3):
+                total = inverse_ref[i, 0] * rhs_ref[source]
+                total = total + inverse_ref[i, 1] * rhs_ref[loads + source]
+                total = total + inverse_ref[i, 2] * rhs_ref[2 * loads + source]
+                base[half * planes + i * few + q] = total
+                x[0, half * planes + i * few + q, 8 : 8 + height, :] = total
+            return carry
+
+        lax.fori_loop(0, few, one, 0)
+
+    def pack(slot, step, half):
+        own = slice(half * planes, (half + 1) * planes)
+        sent[step, half, 0, :planes, :] = x[slot, own, 8, :]
+        sent[step, half, 1, :planes, :] = x[slot, own, 7 + height, :]
 
         def columns(p, carry):
             left, right = carry
-            plane = x[slot, p, 8 : 8 + height, :]
+            plane = x[slot, half * planes + p, 8 : 8 + height, :]
             left = jnp.where(lane == p, pltpu.roll(plane, p, 1), left)
             right = jnp.where(lane == p, pltpu.roll(plane, p + 1, 1), right)
             return left, right
 
         blank = jnp.zeros((height, LANES), jnp.float32)
         left, right = lax.fori_loop(0, planes, columns, (blank, blank), unroll=4)
-        sent[step, 2, :height, :] = left
-        sent[step, 3, :height, :] = right
-
-    def copies(step, d):
+        sent[step, half, 2, :height, :] = left
+        sent[step, half, 3, :height, :] = right
+
+    def copy(step, half, d, side):
         return pltpu.make_async_remote_copy(
-            src_ref=sent.at[step, d],
-            dst_ref=halo.at[step, d ^ 1],
-            send_sem=send_sem.at[step, d],
-            recv_sem=recv_sem.at[step, d ^ 1],
+            src_ref=sent.at[step, half, d, pl.ds(0, extent[d])],
+            dst_ref=halo.at[step, half, side, pl.ds(0, extent[d])],
+            send_sem=send_sem.at[step, half, d],
+            recv_sem=recv_sem.at[step, half, side],
             device_id=peers[d],
             device_id_type=MESH,
         )
 
-    def receives(step, d):
-        return pltpu.make_async_remote_copy(
-            src_ref=sent.at[step, d],
-            dst_ref=halo.at[step, d],
-            send_sem=send_sem.at[step, d],
-            recv_sem=recv_sem.at[step, d],
-            device_id=peers[d],
-            device_id_type=MESH,
-        )
-
-    pack(0, 0)
+    def start(step, half):
+        for d in range(4):
+
+            @pl.when(exists[d])
+            def _():
+                copy(step, half, d, d ^ 1).start()
+
+    def fold(d, carry):
+        on = pattern_ref[d].astype(jnp.float32)
+        for k in range(3):
+            column = [blocks_ref[d, j, k] * on for j in range(3)]
+            for i in range(3):
+                total = inverse_ref[i, 0] * column[0]
+                total = total + inverse_ref[i, 1] * column[1]
+                mixed[d, i, k] = total + inverse_ref[i, 2] * column[2]
+        return carry
+
+    first(0)
+    pack(0, 0, 0)
     present = sum(e.astype(jnp.int32) for e in exists)
     pl.semaphore_wait(barrier, present)
+    start(0, 0)
+    for half in range(1, HALVES):
+        first(half)
+        pack(0, 0, half)
+        start(0, half)
+    lax.fori_loop(0, 4, fold, 0)
     for step in range(ITERS - 1):
         old = step % 2
-        for d in range(4):
-
-            @pl.when(exists[d])
-            def _():
-                copies(step, d).start()
-
-        if step == 0:
-
-            def fold(d, carry):
-                on = pattern_ref[d].astype(jnp.float32)
+        last = step == ITERS - 2
+        for half in range(HALVES):
+            for d in range(4):
+
+                @pl.when(exists[d])
+                def _():
+                    copy(step, half, d, d).wait_send()
+                    copy(step, half, d, d).wait_recv()
+
+            own = slice(half * planes, (half + 1) * planes)
+            x[old, own, 7, :] = halo[step, half, 0, :planes, :]
+            x[old, own, 8 + height, :] = halo[step, half, 1, :planes, :]
+
+            def update(q, carry):
+                totals = [base[half * planes + i * few + q] for i in range(3)]
                 for k in range(3):
-                    column = [blocks_ref[d, j, k] * on for j in range(3)]
-                    for i in range(3):
-                        total = inverse_ref[i, 0] * column[0]
-                        total = total + inverse_ref[i, 1] * column[1]
-                        mixed[d, i, k] = total + inverse_ref[i, 2] * column[2]
+                    local = k * few + q
+                    p = half * planes + local
+                    plane = x[old, p, 8 : 8 + height, :]
+                    left = jnp.where(
+                        lane == 0,
+                        pltpu.roll(halo[step, half, 2, :height, :], lax.rem(LANES - local, LANES), 1),
+                        pltpu.roll(plane, 1, 1),
+                    )
+                    right = jnp.where(
+                        lane == LANES - 1,
+                        pltpu.roll(halo[step, half, 3, :height, :], LANES - 1 - local, 1),
+                        pltpu.roll(plane, LANES - 1, 1),
+                    )
+                    shifted = (x[old, p, 7 : 7 + height, :], x[old, p, 9 : 9 + height, :], left, right)
+                    for d in range(4):
+                        for i in range(3):
+                            totals[i] = totals[i] - mixed[d, i, k] * shifted[d]
+                for i in range(3):
+                    if last:
+                        planes_ref[i * loads + half * few + q] = totals[i]
+                    else:
+                        x[1 - old, half * planes + i * few + q, 8 : 8 + height, :] = totals[i]
                 return carry
 
-            lax.fori_loop(0, 4, fold, 0)
-        for d in range(4):
-
-            @pl.when(exists[d])
-            def _():
-                copies(step, d).wait_send()
-                receives(step, d).wait_recv()
-
-        x[old, :, 7, :] = halo[step, 0]
-        x[old, :, 8 + height, :] = halo[step, 1]
-        last = step == ITERS - 2
-
-        def update(q, carry):
-            totals = [base[i * loads + q] for i in range(3)]
-            for k in range(3):
-                p = k * loads + q
-                plane = x[old, p, 8 : 8 + height, :]
-                left = jnp.where(
-                    lane == 0, pltpu.roll(halo[step, 2, :height, :], lax.rem(LANES - p, LANES), 1), pltpu.roll(plane, 1, 1)
-                )
-                right = jnp.where(
-                    lane == LANES - 1,
-                    pltpu.roll(halo[step, 3, :height, :], LANES - 1 - p, 1),
-                    pltpu.roll(plane, LANES - 1, 1),
-                )
-                shifted = (x[old, p, 7 : 7 + height, :], x[old, p, 9 : 9 + height, :], left, right)
-                for d in range(4):
-                    for i in range(3):
-                        totals[i] = totals[i] - mixed[d, i, k] * shifted[d]
-            for i in range(3):
-                if last:
-                    out_ref[q, i] = totals[i]
-                    planes_ref[i * loads + q] = totals[i]
-                else:
-                    x[1 - old, i * loads + q, 8 : 8 + height, :] = totals[i]
-            return carry
-
-        lax.fori_loop(0, loads, update, 0)
-        if not last:
-            pack(1 - old, step + 1)
+            lax.fori_loop(0, few, update, 0)
+            if not last:
+                pack(1 - old, step + 1, half)
+                start(step + 1, half)
 
 
 def sweeps(rhs, inverse, blocks, pattern, row_count, col_count, loads):
     height = inverse.shape[2]
     planes = 3 * loads
     steps = ITERS - 1
-    span = max(planes, height)
+    span = max(planes // HALVES, height)
     return pl.pallas_call(
         functools.partial(sweep_kernel, row_count, col_count, loads),
         in_specs=[spec_vmem()] * 4,
-        out_specs=(spec_vmem(), spec_vmem()),
-        out_shape=(
-            jax.ShapeDtypeStruct((loads, 3, height, LANES), jnp.float32),
-            jax.ShapeDtypeStruct((planes, height, LANES), jnp.float32),
-        ),
+        out_specs=spec_vmem(),
+        out_shape=jax.ShapeDtypeStruct((planes, height, LANES), jnp.float32),
         scratch_shapes=[
             pltpu.VMEM((planes, height, LANES), jnp.float32),
             pltpu.VMEM((2, planes, height + 16, LANES), jnp.float32),
             pltpu.VMEM((4, 3, 3, height, LANES), jnp.float32),
-            pltpu.VMEM((steps, 4, span, LANES), jnp.float32),
-            pltpu.VMEM((steps, 4, span, LANES), jnp.float32),
-            pltpu.SemaphoreType.DMA((steps, 4)),
-            pltpu.SemaphoreType.DMA((steps, 4)),
+            pltpu.VMEM((steps, HALVES, 4, span, LANES), jnp.float32),
+            pltpu.VMEM((steps, HALVES, 4, span, LANES), jnp.float32),
+            pltpu.SemaphoreType.DMA((steps, HALVES, 4)),
+            pltpu.SemaphoreType.DMA((steps, HALVES, 4)),
         ],
         compiler_params=pltpu.CompilerParams(
             vmem_limit_bytes=VMEM_LIMIT, collective_id=0, has_side_effects=True
@@ -539,8 +558,8 @@
     ).reshape(-1)
     received = restrict(fine_residual, restriction, restriction_pattern, devices, col_count)
     rhs = gather(slots, received, devices, loads, height)
-    iterate, planes = sweeps(rhs, block_inverse, off_blocks, operator_pattern, row_count, col_count, loads)
-    table = scatter(slots, planes.reshape(-1, LANES), loads)
+    planes = sweeps(rhs, block_inverse, off_blocks, operator_pattern, row_count, col_count, loads)
+    table, iterate = scatter(slots, planes.reshape(-1, LANES), loads)
     arrived = pack_send(table, devices, col_count, loads).reshape(-1, LANES)
     fine_correction = prolong(arrived, restriction, restriction_pattern, devices, loads)
     return (iterate, fine_correction)

time: 129 us -> 125 us (0.969)
  Pallas kernels: 125 us -> 122 us
    pallas_call x1, Pallas kernels: 24.3 us -> 20.7 us  [sweeps(): pl.pallas_call(functools.partial(sweep_kernel, row_count, col_count, load...]
where the time goes in v2:
time: 125 us; the launch traced here: 124 us
  Pallas kernels  122 us (98%)
  other arithmetic  1.43 us (1%)
    pallas_call x1, Pallas kernels, restrict(): pl.pallas_call(functools.partial(restrict_kernel, devices, col_count, loa...  35.6 us
    pallas_call x1, Pallas kernels, pack_send(): pl.pallas_call(functools.partial(pack_kernel, devices, col_count, loads),...  35.1 us
    pallas_call x1, Pallas kernels, sweeps(): pl.pallas_call(functools.partial(sweep_kernel, row_count, col_count, load...  20.7 us
    pallas_call x1, Pallas kernels, gather(): pl.pallas_call(functools.partial(gather_kernel, devices, loads), in_specs...  12 us
    pallas_call x1, Pallas kernels, scatter(): pl.pallas_call(functools.partial(scatter_kernel, loads), in_specs=[pl.Blo...  10.2 us
    pallas_call x1, Pallas kernels, prolong(): pl.pallas_call(functools.partial(prolong_kernel, devices, loads), grid=(F...  8.47 us

profile of v2, /device:TPU:1, one launch (start us, length us, event | category | flops | bytes accessed | tf_op | source)
XLA Modules:
  0.0 124.0 jit_solution(10352988981898522744)
XLA Ops:
  0.6 1.4 %fusion.4.slots_ref = s32[6144]{0:T(1024)} fusion(s32[48,128]{1,0:T(8,128)} %param.10), kind=kLoop, calls=%fused_computation.20 | loop fusion | flops 436224 | bytes 49152 | tf_op jit(solution)/shard_map/reshape | solution.py:558
  2.1 35.6 %restrict_send.1.chunk_ref = f32[3,32,24,128]{3,2,1,0:T(8,128)} custom-call(f32[3,16,49152]{2,1,0:T(8,128)} %bitcast.9, f32[3,16,49152]{2,1,0:T(8,128)} %bitcast.10, f32[3,16,49152]{2,1,0:T(8,128)} %bitcast.11, f32[3,16,49152]{2,1,0:T(8,128)} %bitcast.12, f32[3,16,49152]{2,1,0:T(8,128)} %bitcast.13, f32[3,16,49152]{2,1,0:T(8,128)} %bitcast.14, ...), custom_call_target="tpu_custom_call" | custom-call | tf_op jit(solution)/shard_map/restrict_send/pallas_call | solution.py:122
  37.6 12.0 %gather_cells.1 = f32[2304,128]{1,0:T(8,128)} custom-call(s32[6144]{0:T(1024)} %fusion.4.slots_ref, f32[3,32,24,128]{3,2,1,0:T(8,128)} %restrict_send.1.chunk_ref), custom_call_target="tpu_custom_call" | custom-call | tf_op jit(solution)/shard_map/gather_cells/pallas_call | solution.py:182
  49.6 20.7 %sweeps.1 = f32[48,48,128]{2,1,0:T(8,128)} custom-call(f32[48,48,128]{2,1,0:T(8,128)} %bitcast.29, f32[3,3,48,128]{3,2,1,0:T(8,128)} %inverse_ref.1, f32[4,3,3,48,128]{4,3,2,1,0:T(8,128)} %blocks_ref.1, s32[4,48,128]{2,1,0:T(8,128)} %pattern_ref.1), custom_call_target="tpu_custom_call" | custom-call | tf_op jit(solution)/shard_map/sweeps/pallas_call | solution.py:467
  70.3 10.2 %scatter_cells.1 = (f32[6144,128]{1,0:T(8,128)}, f32[16,3,48,128]{3,2,1,0:T(8,128)}) custom-call(s32[6144]{0:T(1024)} %fusion.4.slots_ref, f32[2304,128]{1,0:T(8,128)} %bitcast.28), custom_call_target="tpu_custom_call" | custom-call | tf_op jit(solution)/shard_map/scatter_cells/pallas_call | solution.py:221
  80.5 35.1 %pack_send.1 = f32[32,72,128]{2,1,0:T(8,128)} custom-call(f32[6144,128]{1,0:T(8,128)} %get-tuple-element.5.table), custom_call_target="tpu_custom_call" | custom-call | tf_op jit(solution)/shard_map/pack_send/pallas_call | solution.py:291
  115.6 8.5 %prolong.1 = f32[3,16,49152]{2,1,0:T(8,128)} custom-call(f32[2304,128]{1,0:T(8,128)} %bitcast.27, f32[3,3,49152]{2,1,0:T(4,128)} %restriction_ref.1, s32[384,128]{1,0:T(8,128)} %bitcast.25), custom_call_target="tpu_custom_call" | custom-call | tf_op jit(solution)/shard_map/prolong/pallas_call | solution.py:517
